TPU v7x, 32 devices: a 4x4x1 block of a 4x4x8 slice. The times are simulated.
32 devices in a mesh: dp: 1 (over z), tp: 4 (over y), pp: 8 (over x, core).
Axes of the slice: x: 4, y: 4, z: 1, core: 2. Of those that a mesh axis runs over, the one named last changes fastest.
The devices are a block of a 4x4x8 slice.
Arguments:
- x_in: bfloat16 [16, 8, 128, 1024], P(None, 'dp', 'tp')
- ln_params: float32 [8, 4, 1024], P('pp')
- w_q: bfloat16 [8, 1024, 16, 1, 64], P('pp', None, 'tp')
- w_k: bfloat16 [8, 1024, 16, 64], P('pp', None, 'tp')
- w_v: bfloat16 [8, 1024, 16, 64], P('pp', None, 'tp')
- w_o: bfloat16 [8, 16, 1, 64, 1024], P('pp', 'tp')
- w_up: bfloat16 [8, 1024, 4096], P('pp', None, 'tp')
- w_down: bfloat16 [8, 4096, 1024], P('pp', 'tp')
Outputs:
- output: bfloat16 [8, 16, 8, 128, 1024], P('pp', None, 'dp', 'tp')
All inputs are finite; a program needn't handle non-finite values.
Results may differ from a plain program's by a relative error of at most 0.02.
Values are sent between devices in bfloat16 or wider.
A program may use at most 768 MiB of HBM per device.

v0:
```python
import functools

import jax
import jax.numpy as jnp
import numpy as np
from jax import lax
from jax.experimental import pallas as pl
from jax.experimental.pallas import tpu as pltpu
from jax.sharding import PartitionSpec as P

LN_EPS = 1e-5
ROPE_BASE = 10000.0
F32, BF16 = jnp.float32, jnp.bfloat16
MESH = pl.DeviceIdType.MESH
DETOURS = ((128, 0, 2, 4), (160, 0, 1, 6), (64, 2, 1, 2))
EARLY_MICRO = 8
HAND_AT, HANDED_AT = 8, 14


def rope_tables(seq_len, head_dim, heads):
    half = head_dim // 2
    inv_freq = (ROPE_BASE ** (-2.0 * np.arange(half) / head_dim)).astype(np.float32)
    angles = np.arange(seq_len, dtype=np.float32)[:, None] * inv_freq[None, :]
    cos = np.tile(np.cos(angles.astype(np.float64)), (1, heads)).astype(np.float32)
    sin = np.tile(np.sin(angles.astype(np.float64)), (1, heads)).astype(np.float32)
    scale = np.float32(head_dim ** -0.5)
    return np.stack([cos * scale, sin * scale, cos, sin])


def head_masks(head_dim, heads):
    half = head_dim // 2
    lanes = np.arange(heads * head_dim)
    roped = np.stack([(lanes % (heads * half)) // half == head for head in range(heads)])
    plain = np.stack([lanes // head_dim == head for head in range(heads)])
    return np.stack([roped, plain]).astype(np.float32)


def dot(lhs, rhs):
    return jnp.dot(lhs, rhs, preferred_element_type=F32)


def layer_norms(x, ln_ref, h_attn, h_mlp):
    x_f32 = x.astype(F32)
    centred = x_f32 - jnp.mean(x_f32, axis=-1, keepdims=True)
    variance = jnp.mean(centred * centred, axis=-1, keepdims=True)
    normed = centred * lax.rsqrt(variance + LN_EPS)
    h_attn[...] = (normed * ln_ref[0:1, :] + ln_ref[1:2, :]).astype(BF16)
    h_mlp[...] = (normed * ln_ref[2:3, :] + ln_ref[3:4, :]).astype(BF16)


def roped(first, second, cos, sin):
    return jnp.concatenate([first * cos - second * sin, second * cos + first * sin], axis=1).astype(BF16)


def causal_softmax(scores, allowed):
    masked = jnp.where(allowed, scores, -1e30)
    weight = jnp.exp(masked - jnp.max(masked, axis=1, keepdims=True))
    return (weight * (1.0 / jnp.sum(weight, axis=1, keepdims=True))).astype(BF16)


def gelu_of_half(half_x):
    return (half_x * (1.0 + lax.erf(half_x * np.float32(2.0 ** 0.5)))).astype(BF16)


def add_layer(heads, shards, h_attn, h_mlp, acc, w_qkv, w_up, w_out, rope, masks, mixed, x=None, y=None, fresh=True, before_last_out=None):
    seq_len, d_model = acc.shape
    width = w_qkv.shape[2] // 3
    half = width // 2
    cols = d_model // heads
    hidden = w_up.shape[2] // heads
    allowed = lax.broadcasted_iota(jnp.int32, (seq_len, seq_len), 0) >= lax.broadcasted_iota(jnp.int32, (seq_len, seq_len), 1)
    raw, ups, score_pairs, probs = {}, {}, {}, {}

    def project(turn, which):
        if turn < len(shards):
            raw[which] = dot(h_attn[...], w_qkv[shards[turn], :, which * width:(which + 1) * width])

    def score(pair):
        k_pair = jnp.concatenate([raw[1] * masks[0, h:h + 1, :] for h in (2 * pair, 2 * pair + 1)], axis=0)
        score_pairs[pair] = lax.dot_general(raw[0], k_pair, (((1,), (1,)), ((), ())), preferred_element_type=F32)

    def soften(head):
        side = head % 2 * seq_len
        probs[head] = causal_softmax(score_pairs[head // 2][:, side:side + seq_len], allowed)

    def context(turn):
        v_heads = jnp.concatenate([v * masks[1, h:h + 1, :] for h in range(heads)], axis=0)
        mixed[turn % 2, :, :width] = dot(jnp.concatenate([probs[h] for h in range(heads)], axis=1), v_heads).astype(BF16)

    def up(turn, part):
        ups[part] = dot(h_mlp[...], w_up[shards[turn], :, part * hidden:(part + 1) * hidden])

    def gelu(turn, part):
        mixed[turn % 2, :, width + part * hidden:width + (part + 1) * hidden] = gelu_of_half(ups[part])

    def add_out(turn, part):
        piece = slice(part * cols, (part + 1) * cols)
        term = dot(mixed[turn % 2], w_out[shards[turn], :, piece])
        if turn > 0 or not fresh:
            term += acc[:, piece]
        if y is not None and turn == len(shards) - 1:
            y[:, piece] = (term + x[:, piece].astype(F32)).astype(BF16)
        else:
            acc[:, piece] = term

    for which in range(3):
        project(0, which)
    for turn in range(len(shards)):
        raw[0] = roped(raw[0][:, :half], raw[0][:, half:], rope[0], rope[1])
        raw[1] = roped(raw[1][:, :half], raw[1][:, half:], rope[2], rope[3])
        v = raw[2].astype(BF16)
        score(0)
        if turn == 0:
            score(1)
            for head in range(heads):
                up(turn, head)
                if head > 0:
                    gelu(turn, head - 1)
                soften(head)
            project(turn + 1, 0)
            project(turn + 1, 1)
            gelu(turn, 3)
            context(turn)
            project(turn + 1, 2)
        else:
            add_out(turn - 1, 0)
            score(1)
            for head in range(heads):
                soften(head)
                if head < 3:
                    add_out(turn - 1, head + 1)
            up(turn, 0)
            up(turn, 1)
            gelu(turn, 0)
            context(turn)
            up(turn, 2)
            gelu(turn, 1)
            up(turn, 3)
            gelu(turn, 2)
            project(turn + 1, 0)
            gelu(turn, 3)
            project(turn + 1, 1)
            project(turn + 1, 2)
    if before_last_out is not None:
        before_last_out()
    for part in range(heads):
        add_out(len(shards) - 1, part)


def kernel(tp_size, pp_size, heads, x_hbm, ln_hbm, wq_hbm, wk_hbm, wv_hbm, wo_hbm, wup_hbm, wdown_hbm, rope_hbm, masks_hbm, out,
           w_qkv, w_up, w_out, raw, detour, xs, ys, ln_half, rope, masks, h_attn, h_mlp, acc, mixed,
           load_sem, w_send, near_recv, far_recv, d_send, d_in, d_out, x_send, x_recv, x_local, x_hand, pp_send, pp_recv, o_send, o_recv):
    me = lax.axis_index("tp")
    stage = lax.axis_index("pp")
    right, left = lax.rem(me + 1, tp_size), lax.rem(me + tp_size - 1, tp_size)
    far = lax.rem(me + 2, tp_size)
    nxt = lax.rem(stage + 1, pp_size)
    last_stage = pp_size - 1
    num_micro, num_seq, seq_len, d_model = xs.shape
    tokens = seq_len // tp_size
    width = raw.shape[1]

    loads = [
        pltpu.make_async_copy(wup_hbm, w_up.at[me], load_sem.at[0]),
        pltpu.make_async_copy(wq_hbm, raw.at[0], load_sem.at[1]),
        pltpu.make_async_copy(wk_hbm, raw.at[1], load_sem.at[2]),
        pltpu.make_async_copy(wv_hbm, raw.at[2], load_sem.at[3]),
        pltpu.make_async_copy(wo_hbm, w_out.at[me, pl.ds(0, width)], load_sem.at[4]),
        pltpu.make_async_copy(wdown_hbm, w_out.at[me, pl.ds(width, wdown_hbm.shape[0])], load_sem.at[5]),
        pltpu.make_async_copy(ln_hbm, ln_half, load_sem.at[6]),
        pltpu.make_async_copy(rope_hbm, rope, load_sem.at[7]),
        pltpu.make_async_copy(masks_hbm, masks, load_sem.at[8]),
    ]
    for load in loads:
        load.start()

    barrier = pltpu.get_barrier_semaphore()

    def knock(index, _):
        peer = {"tp": index // pp_size, "pp": lax.rem(index, pp_size)}
        pl.semaphore_signal(barrier, inc=1, device_id=peer, device_id_type=MESH)
        return 0
    lax.fori_loop(0, tp_size * pp_size, knock, 0)
    pl.semaphore_wait(barrier, tp_size * pp_size)

    def token_rows(owner):
        return pl.ds(pl.multiple_of(owner * tokens, tokens), tokens)

    def seq_rows(owner):
        return pl.ds(owner * num_seq, num_seq)

    early = (stage == last_stage, 0, EARLY_MICRO)
    late = (stage == last_stage - 4, EARLY_MICRO, num_micro - EARLY_MICRO)

    def collect(group):
        micros = pl.ds(group[1], group[2])
        pltpu.make_async_copy(x_hbm.at[micros, seq_rows(me)], ys.at[micros, :, token_rows(me), :], x_local).start()
        for step in range(1, tp_size):
            peer = lax.rem(me + step, tp_size)
            pltpu.make_async_remote_copy(
                src_ref=x_hbm.at[micros, seq_rows(peer)], dst_ref=ys.at[micros, :, token_rows(me), :],
                send_sem=x_send, recv_sem=x_recv, device_id={"tp": peer}, device_id_type=MESH).start()

    def take_blocks(sem, blocks):
        seqs = blocks * num_seq // tp_size
        take(sem, ys.at[pl.ds(0, seqs // num_seq)] if seqs % num_seq == 0 else ys.at[pl.ds(0, seqs), 0])

    def hand_on(group):
        take_blocks(x_local, group[2])
        take_blocks(x_recv, group[2] * (tp_size - 1))

        def one(index, _):
            micro = group[1] + index
            for seq in range(num_seq):
                pltpu.make_async_remote_copy(
                    src_ref=ys.at[micro, seq], dst_ref=xs.at[micro, seq], send_sem=x_hand,
                    recv_sem=pp_recv.at[micro, seq], device_id={"pp": 0}, device_id_type=MESH).start()
            return 0
        lax.fori_loop(0, group[2], one, 0)

    def handed(group):
        take_blocks(x_hand, group[2] * tp_size)
        take_blocks(x_send, group[2] * (tp_size - 1))

    def pp_copy(micro, seq):
        return pltpu.make_async_remote_copy(
            src_ref=ys.at[micro, seq], dst_ref=xs.at[micro, seq], send_sem=pp_send,
            recv_sem=pp_recv.at[micro, seq], device_id={"pp": nxt}, device_id_type=MESH)

    @pl.when(early[0])
    def _():
        collect(early)

    parts = [(w_up, 0, w_up.shape[1], (0, 0)), (w_qkv, 0, w_qkv.shape[1], (0, 0))]
    detour_parts = []
    start = 0
    for rows, first, count, later in DETOURS:
        detour_parts.append((len(detour_parts), pl.ds(start, rows), first, first + count, later))
        parts.append((w_out, start, rows, (first, first + count)))
        start += rows
    parts.append((w_out, start, w_out.shape[1] - start, (0, 0)))
    chunks = [(ref, start + side * rows // 2, rows // 2) for ref, start, rows, _ in parts for side in range(2)]

    def on_ring(part, action):
        first, end = parts[part][3]
        if end > first:
            pl.when((stage < first) | (stage >= end))(action)
        else:
            action()

    def shard_copy(index, owner, send_sem, recv_sem, peer):
        ref, start, rows = chunks[index]
        piece = ref.at[owner, pl.ds(start, rows)]
        return pltpu.make_async_remote_copy(
            src_ref=piece, dst_ref=piece, send_sem=send_sem, recv_sem=recv_sem, device_id={"tp": peer}, device_id_type=MESH)

    def own_copy(index, way):
        return shard_copy(index, me, w_send, near_recv.at[way, index], right if way == 0 else left)

    def near_copy(index, way):
        return shard_copy(index, left if way == 0 else right, w_send, near_recv.at[way, index],
                          right if way == 0 else left)

    def fwd_copy(index):
        way = index % 2
        return shard_copy(index, left if way == 0 else right, w_send, far_recv.at[index // 2],
                          right if way == 0 else left)

    def take(sem, *refs):
        for ref in refs:
            pltpu.make_async_copy(ref, ref, sem).wait()

    def send_own(part):
        def send():
            for way in range(2):
                own_copy(2 * part + way, way).start()
            for way in range(2):
                own_copy(2 * part + 1 - way, way).start()
        on_ring(part, send)

    def pass_on(part):
        def forward():
            for way in range(2):
                near_copy(2 * part + way, way).wait_recv()
                fwd_copy(2 * part + way).start()
        on_ring(part, forward)

    def take_near(part):
        def wait():
            for way in range(2):
                near_copy(2 * part + 1 - way, way).wait_recv()
        on_ring(part, wait)

    def take_far(part):
        ref, start, rows, _ = parts[part]
        on_ring(part, lambda: take(far_recv.at[part], ref.at[far, pl.ds(start, rows)]))

    def send_detours():
        for part, piece, first, end, later in detour_parts:
            @pl.when((stage >= first) & (stage < end))
            def _():
                for step in range(1, tp_size):
                    pltpu.make_async_remote_copy(
                        src_ref=w_out.at[me, piece], dst_ref=detour.at[step - 1, piece],
                        send_sem=w_send, recv_sem=d_in.at[part],
                        device_id={"tp": lax.rem(me + step, tp_size), "pp": stage + later}, device_id_type=MESH).start()

    def pass_detours():
        for part, piece, first, end, later in detour_parts:
            @pl.when((stage >= first + later) & (stage < end + later))
            def _():
                take(d_in.at[part], detour.at[:, piece])
                for step in range(1, tp_size):
                    pltpu.make_async_remote_copy(
                        src_ref=detour.at[step - 1, piece],
                        dst_ref=w_out.at[lax.rem(me + tp_size - step, tp_size), piece],
                        send_sem=d_send.at[part], recv_sem=d_out.at[part],
                        device_id={"pp": stage - later}, device_id_type=MESH).start()

    def take_detours():
        for part, piece, first, end, _ in detour_parts:
            @pl.when((stage >= first) & (stage < end))
            def _():
                take(d_out.at[part], detour.at[:, piece])

    loads[0].wait()
    send_own(0)
    for load in loads[4:6]:
        load.wait()
    send_detours()
    for load in loads[1:4]:
        load.wait()
    head_dim = width // heads
    part = head_dim // 2
    for which in range(3):
        starts = [head * head_dim + side * part for side in range(2) for head in range(heads)]
        if which == 2:
            starts = list(range(0, width, part))
        for col in range(0, d_model, width):
            block = jnp.concatenate([raw[which, start:start + part, col:col + width] for start in starts], axis=0)
            w_qkv[me, col:col + width, which * width:(which + 1) * width] = block.T

    for part in range(1, len(parts)):
        send_own(part)
    for load in loads[6:]:
        load.wait()
    ln_half[2:4, :] = 0.5 * ln_half[2:4, :]
    pass_detours()

    @pl.when(early[0])
    def _():
        hand_on(early)

    for part in range(len(parts)):
        pass_on(part)
    for part in range(len(parts)):
        take_near(part)
    take_detours()

    @pl.when(early[0])
    def _():
        handed(early)

    @pl.when(late[0])
    def _():
        collect(late)

    def o_copy(micro, seq, step):
        peer = lax.rem(me + step, tp_size)
        return pltpu.make_async_remote_copy(
            src_ref=ys.at[micro, seq, token_rows(peer), :], dst_ref=out.at[micro, me * num_seq + seq],
            send_sem=o_send, recv_sem=o_recv, device_id={"tp": peer}, device_id_type=MESH)

    def hand_over(micro, seq):
        @pl.when(stage < last_stage)
        def _():
            pp_copy(micro, seq).start()

    def put_out(micro, seq):
        out[micro, me * num_seq + seq] = ys[micro, seq, token_rows(me), :]
        for step in range(1, tp_size):
            o_copy(micro, seq, step).start()

    work = (h_attn, h_mlp, acc, w_qkv, w_up, w_out, rope, masks, mixed)

    pp_copy(0, 0).wait_recv()
    layer_norms(xs[0, 0], ln_half, h_attn, h_mlp)
    add_layer(heads, [me, left, right], *work)
    take_far(0)
    take_far(1)

    def rest_of_far():
        for part in range(2, len(parts)):
            take_far(part)
    add_layer(heads, [far], *work, xs.at[0, 0], ys.at[0, 0], fresh=False, before_last_out=rest_of_far)
    hand_over(0, 0)

    def unit(index, _):
        micro, seq = index // num_seq, lax.rem(index, num_seq)
        pp_copy(micro, seq).wait_recv()
        put_out((index - 1) // num_seq, lax.rem(index - 1, num_seq))
        layer_norms(xs[micro, seq], ln_half, h_attn, h_mlp)
        add_layer(heads, list(range(tp_size)), *work, xs.at[micro, seq], ys.at[micro, seq])
        hand_over(micro, seq)

        @pl.when(late[0])
        def _():
            pl.when(index == HAND_AT)(lambda: hand_on(late))
            pl.when(index == HANDED_AT)(lambda: handed(late))
        return 0

    lax.fori_loop(1, num_micro * num_seq, unit, 0)
    put_out(num_micro - 1, num_seq - 1)

    take(w_send, w_out, w_up)

    for part, piece, first, end, later in detour_parts:
        @pl.when((stage >= first + later) & (stage < end + later))
        def _():
            take(d_send.at[part], detour.at[:, piece])

    @pl.when(stage < last_stage)
    def _():
        take(pp_send, ys)
    take_blocks(o_send, num_micro * (tp_size - 1))
    take_blocks(o_recv, num_micro * (tp_size - 1))


def solution(mesh):
    tp_size, pp_size = mesh.shape["tp"], mesh.shape["pp"]

    def stage_body(x_in, ln_params, w_q, w_k, w_v, w_o, w_up, w_down):
        num_micro, batch, tokens, d_model = x_in.shape
        heads, head_dim = w_k.shape[2:]
        width = heads * head_dim
        hidden = w_up.shape[2]
        seq_len = tokens * tp_size
        num_seq = batch // tp_size
        rope = jnp.asarray(rope_tables(seq_len, head_dim, heads))
        masks = jnp.asarray(head_masks(head_dim, heads), dtype=BF16)
        wq_t = jnp.transpose(w_q[0], (1, 2, 3, 0)).reshape(width, d_model)
        wk_t = jnp.transpose(w_k[0], (1, 2, 0)).reshape(width, d_model)
        wv_t = jnp.transpose(w_v[0], (1, 2, 0)).reshape(width, d_model)
        vmem = pl.BlockSpec(memory_space=pltpu.VMEM)
        hbm = pl.BlockSpec(memory_space=pl.ANY)
        dma = pltpu.SemaphoreType.DMA
        out = pl.pallas_call(
            functools.partial(kernel, tp_size, pp_size, heads),
            out_shape=pltpu.VMEM(x_in.shape, BF16),
            in_specs=[hbm] * 10,
            out_specs=vmem,
            scratch_shapes=[
                pltpu.VMEM((tp_size, d_model, 3 * width), BF16),
                pltpu.VMEM((tp_size, d_model, hidden), BF16),
                pltpu.VMEM((tp_size, width + hidden, d_model), BF16),
                pltpu.VMEM((3, width, d_model), BF16),
                pltpu.VMEM((tp_size - 1, sum(rows for rows, *_ in DETOURS), d_model), BF16),
                pltpu.VMEM((num_micro, num_seq, seq_len, d_model), BF16),
                pltpu.VMEM((num_micro, num_seq, seq_len, d_model), BF16),
                pltpu.VMEM((4, d_model), F32),
                pltpu.VMEM(rope.shape, F32),
                pltpu.VMEM(masks.shape, BF16),
                pltpu.VMEM((seq_len, d_model), BF16),
                pltpu.VMEM((seq_len, d_model), BF16),
                pltpu.VMEM((seq_len, d_model), F32),
                pltpu.VMEM((2, seq_len, width + hidden), BF16),
                dma((9,)), dma, dma((2, 12)), dma((6,)), dma((3,)), dma((3,)), dma((3,)), dma, dma, dma, dma, dma, dma((num_micro, num_seq)), dma, dma,
            ],
            compiler_params=pltpu.CompilerParams(
                collective_id=0, has_side_effects=True, vmem_limit_bytes=54 * 1024 * 1024),
            name="stage",
        )(x_in, ln_params[0], wq_t, wk_t, wv_t, w_o[0].reshape(width, d_model), w_up[0], w_down[0], rope, masks)
        return out[None]

    in_specs = (P(None, "dp", "tp", None), P("pp", None, None), P("pp", None, "tp", None, None), P("pp", None, "tp", None), P("pp", None, "tp", None), P("pp", "tp", None, None, None), P("pp", None, "tp"), P("pp", "tp", None))
    return jax.shard_map(stage_body, mesh=mesh, in_specs=in_specs, out_specs=P("pp", None, "dp", "tp", None), check_vma=False)
```

profile of v0, /device:TPU:103, one launch (start us, length us, event | category | flops | bytes accessed | tf_op | source)
XLA Modules:
  0.0 410.6 jit_solution(8929608783406847407)
XLA Ops:
  0.0 407.2 %stage.1 = bf16[16,8,32,1024]{3,2,1,0:T(8,128)(2,1)S(1)} custom-call(bf16[16,8,32,1024]{3,2,1,0:T(8,128)(2,1)} %x_hbm.1, f32[4,1024]{1,0:T(4,128)} %bitcast.27, bf16[256,1024]{1,0:T(8,128)(2,1)} %bitcast.23, bf16[256,1024]{1,0:T(8,128)(2,1)} %bitcast.24, bf16[256,1024]{1,0:T(8,128)(2,1)} %bitcast.25, bf16[256,1024]{1,0:T(8,128)(2,1)} %bitcast.26, ...), custom_call_target="tpu_custom_call" | custom-call | tf_op jit(solution)/shard_map/stage/pallas_call | solution.py:447
  407.2 3.4 copy.12
where the time goes:
time: 411 us
  Pallas kernels  407 us (99%)
    pallas_call x1, Pallas kernels, stage_body(): pl.pallas_call(functools.partial(kernel, tp_size, pp_size, heads), out_sh...  407 us

commit v1 on v0

--- a/solution.py
+++ b/solution.py
@@ -13,8 +13,8 @@
 F32, BF16 = jnp.float32, jnp.bfloat16
 MESH = pl.DeviceIdType.MESH
 DETOURS = ((128, 0, 2, 4), (160, 0, 1, 6), (64, 2, 1, 2))
-EARLY_MICRO = 8
-HAND_AT, HANDED_AT = 8, 14
+EARLY_MICRO = 9
+HAND_AT = 10
 
 
 def rope_tables(seq_len, head_dim, heads):
@@ -201,26 +201,24 @@
                 src_ref=x_hbm.at[micros, seq_rows(peer)], dst_ref=ys.at[micros, :, token_rows(me), :],
                 send_sem=x_send, recv_sem=x_recv, device_id={"tp": peer}, device_id_type=MESH).start()
 
-    def take_blocks(sem, blocks):
-        seqs = blocks * num_seq // tp_size
-        take(sem, ys.at[pl.ds(0, seqs // num_seq)] if seqs % num_seq == 0 else ys.at[pl.ds(0, seqs), 0])
+    def take_blocks(sem, micros, blocks):
+        take(sem, ys.at[pl.ds(0, micros), :, pl.ds(0, blocks * tokens), :])
 
     def hand_on(group):
-        take_blocks(x_local, group[2])
-        take_blocks(x_recv, group[2] * (tp_size - 1))
+        take_blocks(x_local, group[2], 1)
+        take_blocks(x_recv, group[2], tp_size - 1)
 
         def one(index, _):
             micro = group[1] + index
             for seq in range(num_seq):
                 pltpu.make_async_remote_copy(
-                    src_ref=ys.at[micro, seq], dst_ref=xs.at[micro, seq], send_sem=x_hand,
+                    src_ref=ys.at[micro, seq], dst_ref=xs.at[micro, seq], send_sem=x_hand.at[micro],
                     recv_sem=pp_recv.at[micro, seq], device_id={"pp": 0}, device_id_type=MESH).start()
             return 0
         lax.fori_loop(0, group[2], one, 0)
 
-    def handed(group):
-        take_blocks(x_hand, group[2] * tp_size)
-        take_blocks(x_send, group[2] * (tp_size - 1))
+    def handed(micro):
+        take(x_hand.at[micro], ys.at[micro])
 
     def pp_copy(micro, seq):
         return pltpu.make_async_remote_copy(
@@ -359,7 +357,8 @@
 
     @pl.when(early[0])
     def _():
-        handed(early)
+        for micro in range(EARLY_MICRO):
+            handed(micro)
 
     @pl.when(late[0])
     def _():
@@ -406,7 +405,7 @@
         @pl.when(late[0])
         def _():
             pl.when(index == HAND_AT)(lambda: hand_on(late))
-            pl.when(index == HANDED_AT)(lambda: handed(late))
+            pl.when((seq == num_seq - 1) & (micro >= EARLY_MICRO - 1) & (micro < num_micro - 1))(lambda: handed(micro + 1))
         return 0
 
     lax.fori_loop(1, num_micro * num_seq, unit, 0)
@@ -419,11 +418,16 @@
         def _():
             take(d_send.at[part], detour.at[:, piece])
 
+    for group in (early, late):
+        @pl.when(group[0])
+        def _():
+            take_blocks(x_send, group[2], tp_size - 1)
+
     @pl.when(stage < last_stage)
     def _():
         take(pp_send, ys)
-    take_blocks(o_send, num_micro * (tp_size - 1))
-    take_blocks(o_recv, num_micro * (tp_size - 1))
+    take_blocks(o_send, num_micro, tp_size - 1)
+    take_blocks(o_recv, num_micro, tp_size - 1)
 
 
 def solution(mesh):
@@ -464,7 +468,7 @@
                 pltpu.VMEM((seq_len, d_model), BF16),
                 pltpu.VMEM((seq_len, d_model), F32),
                 pltpu.VMEM((2, seq_len, width + hidden), BF16),
-                dma((9,)), dma, dma((2, 12)), dma((6,)), dma((3,)), dma((3,)), dma((3,)), dma, dma, dma, dma, dma, dma((num_micro, num_seq)), dma, dma,
+                dma((9,)), dma, dma((2, 12)), dma((6,)), dma((3,)), dma((3,)), dma((3,)), dma, dma, dma, dma((num_micro,)), dma, dma((num_micro, num_seq)), dma, dma,
             ],
             compiler_params=pltpu.CompilerParams(
                 collective_id=0, has_side_effects=True, vmem_limit_bytes=54 * 1024 * 1024),

time: 411 us -> 393 us (0.956)
  Pallas kernels: 407 us -> 390 us
    pallas_call x1, Pallas kernels: 407 us -> 390 us  [stage_body(): pl.pallas_call(functools.partial(kernel, tp_size, pp_size, heads), out_sh...]
where the time goes in v1:
time: 393 us
  Pallas kernels  390 us (99%)
    pallas_call x1, Pallas kernels, stage_body(): pl.pallas_call(functools.partial(kernel, tp_size, pp_size, heads), out_sh...  390 us

profile of v1, /device:TPU:103, one launch (start us, length us, event | category | flops | bytes accessed | tf_op | source)
XLA Modules:
  0.0 393.3 jit_solution(14563922218829501894)
XLA Ops:
  0.0 389.9 %stage.1 = bf16[16,8,32,1024]{3,2,1,0:T(8,128)(2,1)S(1)} custom-call(bf16[16,8,32,1024]{3,2,1,0:T(8,128)(2,1)} %x_hbm.1, f32[4,1024]{1,0:T(4,128)} %bitcast.27, bf16[256,1024]{1,0:T(8,128)(2,1)} %bitcast.23, bf16[256,1024]{1,0:T(8,128)(2,1)} %bitcast.24, bf16[256,1024]{1,0:T(8,128)(2,1)} %bitcast.25, bf16[256,1024]{1,0:T(8,128)(2,1)} %bitcast.26, ...), custom_call_target="tpu_custom_call" | custom-call | tf_op jit(solution)/shard_map/stage/pallas_call | solution.py:451
  389.9 3.4 copy.12

commit v2 on v1

--- a/solution.py
+++ b/solution.py
@@ -30,9 +30,9 @@
 def head_masks(head_dim, heads):
     half = head_dim // 2
     lanes = np.arange(heads * head_dim)
-    roped = np.stack([(lanes % (heads * half)) // half == head for head in range(heads)])
-    plain = np.stack([lanes // head_dim == head for head in range(heads)])
-    return np.stack([roped, plain]).astype(np.float32)
+    roped, plain = lanes % (heads * half) // half, lanes // head_dim
+    rows = [roped // 2 == 0, roped // 2 == 1, roped % 2 == 0, roped % 2 == 1, plain % 2 == 0, plain % 2 == 1]
+    return np.stack(rows).astype(np.float32)
 
 
 def dot(lhs, rhs):
@@ -75,17 +75,22 @@
         if turn < len(shards):
             raw[which] = dot(h_attn[...], w_qkv[shards[turn], :, which * width:(which + 1) * width])
 
-    def score(pair):
-        k_pair = jnp.concatenate([raw[1] * masks[0, h:h + 1, :] for h in (2 * pair, 2 * pair + 1)], axis=0)
-        score_pairs[pair] = lax.dot_general(raw[0], k_pair, (((1,), (1,)), ((), ())), preferred_element_type=F32)
+    def two(value, mask):
+        return jnp.concatenate([value * masks[mask:mask + 1, :], value * masks[mask + 1:mask + 2, :]], axis=0)
+
+    def score():
+        pairs = lax.dot_general(two(raw[0], 0), two(raw[1], 2), (((1,), (1,)), ((), ())), preferred_element_type=F32)
+        score_pairs[0], score_pairs[1] = pairs[:seq_len], pairs[seq_len:]
 
     def soften(head):
         side = head % 2 * seq_len
         probs[head] = causal_softmax(score_pairs[head // 2][:, side:side + seq_len], allowed)
 
     def context(turn):
-        v_heads = jnp.concatenate([v * masks[1, h:h + 1, :] for h in range(heads)], axis=0)
-        mixed[turn % 2, :, :width] = dot(jnp.concatenate([probs[h] for h in range(heads)], axis=1), v_heads).astype(BF16)
+        pairs = jnp.concatenate([jnp.concatenate([probs[h], probs[h + 1]], axis=1) for h in (0, 2)], axis=0)
+        both = dot(pairs, two(v, 4))
+        mixed[turn % 2, :, :half] = both[:seq_len, :half].astype(BF16)
+        mixed[turn % 2, :, half:width] = both[seq_len:, half:].astype(BF16)
 
     def up(turn, part):
         ups[part] = dot(h_mlp[...], w_up[shards[turn], :, part * hidden:(part + 1) * hidden])
@@ -109,9 +114,8 @@
         raw[0] = roped(raw[0][:, :half], raw[0][:, half:], rope[0], rope[1])
         raw[1] = roped(raw[1][:, :half], raw[1][:, half:], rope[2], rope[3])
         v = raw[2].astype(BF16)
-        score(0)
+        score()
         if turn == 0:
-            score(1)
             for head in range(heads):
                 up(turn, head)
                 if head > 0:
@@ -124,7 +128,6 @@
             project(turn + 1, 2)
         else:
             add_out(turn - 1, 0)
-            score(1)
             for head in range(heads):
                 soften(head)
                 if head < 3:

time: 393 us -> 390 us (level)
  no operation moved by 1% of the time
where the time goes in v2:
time: 390 us
  Pallas kernels  387 us (99%)
    pallas_call x1, Pallas kernels, stage_body(): pl.pallas_call(functools.partial(kernel, tp_size, pp_size, heads), out_sh...  387 us

profile of v2, /device:TPU:103, one launch (start us, length us, event | category | flops | bytes accessed | tf_op | source)
XLA Modules:
  0.0 390.3 jit_solution(15964935039585112000)
XLA Ops:
  0.0 386.9 %stage.1 = bf16[16,8,32,1024]{3,2,1,0:T(8,128)(2,1)S(1)} custom-call(bf16[16,8,32,1024]{3,2,1,0:T(8,128)(2,1)} %x_hbm.1, f32[4,1024]{1,0:T(4,128)} %bitcast.27, bf16[256,1024]{1,0:T(8,128)(2,1)} %bitcast.23, bf16[256,1024]{1,0:T(8,128)(2,1)} %bitcast.24, bf16[256,1024]{1,0:T(8,128)(2,1)} %bitcast.25, bf16[256,1024]{1,0:T(8,128)(2,1)} %bitcast.26, ...), custom_call_target="tpu_custom_call" | custom-call | tf_op jit(solution)/shard_map/stage/pallas_call | solution.py:454
  386.9 3.4 copy.12
